TPU v7x, 32 devices: a whole 2x2x4 slice. The times are simulated.
32 devices in a mesh: parts: 2 (over x), expert: 16 (over z, y, core).
Axes of the slice: x: 2, y: 2, z: 4, core: 2. Of those that a mesh axis runs over, the one named last changes fastest.
Arguments:
- tokens: bfloat16 [2, 128, 7168], P(None, ('parts', 'expert')), parts along dimension 1, may hold values from -6 to 6
- live_rows: int32 [2, 32], P(None, ('parts', 'expert')), parts along dimension 1, may hold values from 3 to 4
- expert_ids: int32 [1, 2, 128, 8], P(None, None, ('parts', 'expert')), parts along dimension 2, may hold values from 0 to 15, all different within a row; in each aligned block of 4 rows (0 to 3, 4 to 7, ..., all dimensions but the last counted through in order) at most 2 rows name the same one
- gate_weights: float32 [1, 2, 128, 8], P(None, None, ('parts', 'expert')), parts along dimension 2, may hold values from 0.25 to 2.5
- norm_gain: float32 [1, 7168], replicated, may hold values from 0.1 to 1.9
- expert_gate_up: bfloat16 [1, 16, 7168, 2048], P(None, 'expert'), may hold values from -0.0625 to 0.0625
- expert_down: bfloat16 [1, 16, 1024, 7168], P(None, 'expert'), may hold values from -0.1875 to 0.1875
- shared_gate_up: bfloat16 [1, 7168, 2048], P(None, 'expert'), may hold values from -0.0625 to 0.0625
- shared_down: bfloat16 [1, 1024, 7168], P(None, None, 'expert'), may hold values from -0.1875 to 0.1875
Outputs:
- hidden_out: bfloat16 [2, 128, 7168], P(None, ('parts', 'expert')), parts along dimension 1
There are 2 independent parts, one for each index of `parts`. A program takes and returns all parts, laid end to end along the dimension named above; an argument that names none is the same for every part. Nothing has to cross between parts.
Inputs may be any that keep to these rules, and one draw needn't show every extreme that they name: `expert_ids`: the 8 ids of a row differ; within the rows of one device for one layer and step, no expert is named by more than 2 rows, a bound that some block reaches.
All inputs are finite; a program needn't handle non-finite values.
Results may differ from a plain program's by a relative error of at most 0.0068.
Values may be sent and summed in bfloat16 or wider, within the bound.
A program may use at most 128 MiB of HBM per device.

v0:
```python
import jax
import jax.numpy as jnp
from jax import lax
from jax.sharding import PartitionSpec as P

EXPERTS = 16


EPSILON = 1e-06


def rms_normed(hidden, gain_row):
    widened = hidden.astype(jnp.float32)
    scaling = lax.rsqrt(jnp.mean(widened * widened, axis=-1, keepdims=True) + EPSILON)
    return (widened * scaling * gain_row).astype(jnp.bfloat16)


def partial_swiglu(inputs, gate_up, down_proj, unit_count):
    projected = jnp.dot(inputs, gate_up, preferred_element_type=jnp.float32)
    activated = (jax.nn.silu(projected[:, :unit_count]) * projected[:, unit_count:]).astype(
        jnp.bfloat16
    )
    return jnp.dot(activated, down_proj, preferred_element_type=jnp.float32)


def slot_tables(id_block, gate_block, is_live, expert_count, capacity):
    row_count, top_count = id_block.shape
    catalog = jnp.arange(expert_count, dtype=jnp.int32)
    hit_mask = ((id_block[:, :, None] == catalog) & is_live[:, None, None]).astype(jnp.int32)
    flat_hits = hit_mask.reshape(row_count * top_count, expert_count)
    earlier = jnp.cumsum(flat_hits, axis=0) - flat_hits
    rank_of = jnp.sum(earlier * flat_hits, axis=1).reshape(row_count, top_count)
    slot_of = jnp.where(is_live[:, None], id_block * capacity + rank_of, -1)
    columns = jnp.arange(expert_count * capacity, dtype=jnp.int32)
    matches = slot_of[:, :, None] == columns
    chooser = jnp.any(matches, axis=1).astype(jnp.bfloat16)
    weights = jnp.sum(jnp.where(matches, gate_block[:, :, None], 0.0), axis=1)
    return (chooser, weights)


def expert_repeat(outgoing, gate_up, down_proj, unit_count, group_size):
    copies = jnp.repeat(outgoing, group_size, axis=0)
    received = lax.all_to_all(copies, "expert", split_axis=0, concat_axis=0, tiled=True)
    flat_rows = received.reshape(received.shape[0] * received.shape[1], received.shape[2])
    results = partial_swiglu(flat_rows, gate_up, down_proj, unit_count).reshape(received.shape)
    returned = lax.all_to_all(results, "expert", split_axis=0, concat_axis=0, tiled=True)
    grouped = returned.reshape(outgoing.shape[0], group_size, returned.shape[1], returned.shape[2])
    return jnp.sum(grouped, axis=1).astype(jnp.bfloat16)


def expert_pass(outgoing, gate_up, down_proj, unit_count, group_size):
    return expert_repeat(outgoing, gate_up, down_proj, unit_count, group_size)


def shared_block(stacked, gate_up_part, down_part, unit_count):
    column_block = lax.all_to_all(stacked, "expert", split_axis=1, concat_axis=0, tiled=True)
    partial_value = jnp.dot(column_block, gate_up_part, preferred_element_type=jnp.float32)
    own_rows = lax.psum_scatter(partial_value, "expert", scatter_dimension=0, tiled=True)
    own_active = (jax.nn.silu(own_rows[:, :unit_count]) * own_rows[:, unit_count:]).astype(
        jnp.bfloat16
    )
    activated = lax.all_gather(own_active, "expert", axis=0, tiled=True)
    own_cols = jnp.dot(activated, down_part, preferred_element_type=jnp.float32).astype(
        jnp.bfloat16
    )
    return lax.all_to_all(own_cols, "expert", split_axis=0, concat_axis=1, tiled=True)


def per_device(
    tokens,
    live_rows,
    expert_ids,
    gate_weights,
    norm_gain,
    expert_gate_up,
    expert_down,
    shared_gate_up,
    shared_down,
):
    step_count, row_count, model_width = tokens.shape
    top_count = expert_ids.shape[3]
    expert_count = EXPERTS
    group_size = lax.axis_size("expert") // expert_count
    capacity = max(2, (row_count * top_count + expert_count - 1) // expert_count)
    unit_count = expert_down.shape[2]
    shared_count = shared_down.shape[1]
    position = jnp.arange(row_count, dtype=jnp.int32)
    is_live = [position < live_rows[step_at, 0] for step_at in range(step_count)]
    hidden = [tokens[step_at] for step_at in range(step_count)]
    normed = [rms_normed(hidden[step_at], norm_gain[0]) for step_at in range(step_count)]
    tables = [
        slot_tables(
            expert_ids[0, step_at],
            gate_weights[0, step_at],
            is_live[step_at],
            expert_count,
            capacity,
        )
        for step_at in range(step_count)
    ]
    outgoing = []
    for step_at in range(step_count):
        placed = jnp.dot(tables[step_at][0].T, normed[step_at], preferred_element_type=jnp.float32)
        outgoing.append(placed.astype(jnp.bfloat16).reshape(expert_count, capacity, model_width))
    gate_up = expert_gate_up[0, 0]
    down_proj = expert_down[0, 0]
    returned = expert_pass(
        jnp.concatenate(outgoing, axis=1), gate_up, down_proj, unit_count, group_size
    )
    returns = [
        returned[:, step_at * capacity : (step_at + 1) * capacity] for step_at in range(step_count)
    ]
    stacked = jnp.concatenate(normed, axis=0)
    shared = shared_block(stacked, shared_gate_up[0], shared_down[0], shared_count)
    updated = []
    for step_at in range(step_count):
        flat_back = (
            returns[step_at].reshape(expert_count * capacity, model_width).astype(jnp.float32)
        )
        combined = jnp.dot(tables[step_at][1], flat_back, precision=lax.Precision.HIGHEST)
        combined = combined + shared[step_at * row_count : (step_at + 1) * row_count].astype(
            jnp.float32
        )
        masked = jnp.where(is_live[step_at][:, None], combined, 0.0)
        updated.append((hidden[step_at].astype(jnp.float32) + masked).astype(jnp.bfloat16))
    return jnp.stack(updated)


def solution(mesh):
    placed = (
        P(None, ("parts", "expert"), None),
        P(None, ("parts", "expert")),
        P(None, None, ("parts", "expert"), None),
        P(None, None, ("parts", "expert"), None),
        P(),
        P(None, "expert", None, None),
        P(None, "expert", None, None),
        P(None, "expert", None),
        P(None, None, "expert"),
    )
    return jax.shard_map(
        per_device,
        mesh=mesh,
        in_specs=placed,
        out_specs=P(None, ("parts", "expert"), None),
        check_vma=False,
    )
```

profile of v0, /device:TPU:0, one launch (start us, length us, event | category | flops | bytes accessed | tf_op | source)
XLA Modules:
  0.0 174.1 jit_solution(5779972843402533301)
XLA Ops:
  6.5 1.0 slice_convert_fusion.3
  7.5 1.1 fusion.25
  8.6 0.1 reshape.177
  8.7 0.5 broadcast.131
  9.2 1.5 reduce.3
  10.8 0.1 reshape.178
  10.9 0.2 fusion.20
  11.1 0.7 pad_maximum_fusion.1
  11.8 7.4 %all-to-all-start.2 = ((bf16[8,16,448]{2,0,1:T(8,128)(2,1)}), bf16[8,16,448]{2,0,1:T(8,128)(2,1)S(1)}, u32[]{:S(2)}, u32[]{:S(2)}) async-start(bf16[8,16,448]{2,0,1:T(8,128)(2,1)} %pad_maximum_fusion.1), calls=%async_computation.2 | async-start | bytes 262144 | tf_op jit(solution)/shard_map/all_to_all | solution.py:56
  19.2 0.7 fusion.46
  20.0 1.3 fusion.47
  21.3 0.6 iota_compare_fusion.5
  22.1 0.1 and.22
  22.3 0.2 select_reduce_fusion.3
  22.6 0.6 iota_compare_fusion.4
  23.3 0.1 and.25
  23.5 0.2 select_reduce_fusion.1
  23.8 0.8 fusion.44
  24.6 0.1 fusion.37
  24.7 1.2 convolution_convert_fusion
  25.9 0.2 reshape.171
  26.1 1.2 convolution_convert_fusion.1
  27.3 0.2 reshape.169
  27.4 1.9 %pad_maximum_fusion = bf16[16,4,7168]{2,1,0:T(4,128)(2,1)} fusion(bf16[16,2,7168]{2,1,0:T(2,128)(2,1)S(1)} %reshape.171, bf16[16,2,7168]{2,1,0:T(2,128)(2,1)S(1)} %reshape.169), kind=kLoop, calls=%fused_computation.19 | loop fusion | flops 1835008 | bytes 1835008 | tf_op jit(solution)/shard_map/concatenate | solution.py:108
  29.4 6.1 %all-to-all-start = ((bf16[16,4,7168]{2,1,0:T(4,128)(2,1)}), bf16[16,4,7168]{2,1,0:T(4,128)(2,1)}, u32[]{:S(2)}, u32[]{:S(2)}) async-start(bf16[16,4,7168]{2,1,0:T(4,128)(2,1)} %pad_maximum_fusion), calls=%async_computation | async-start | bytes 1835008 | tf_op jit(solution)/shard_map/all_to_all | solution.py:43
  35.5 1.4 fusion.12
  36.9 19.3 %all-to-all-done = bf16[16,4,7168]{2,1,0:T(4,128)(2,1)} async-done(((bf16[16,4,7168]{2,1,0:T(4,128)(2,1)}), bf16[16,4,7168]{2,1,0:T(4,128)(2,1)}, u32[]{:S(2)}, u32[]{:S(2)}) %all-to-all-start) | async-done | bytes 917536 | tf_op jit(solution)/shard_map/all_to_all | solution.py:43
  56.3 1.7 reshape.172
  57.9 12.1 %fusion = f32[64,2048]{1,0:T(8,128)S(1)} fusion(bf16[64,7168]{1,0:T(8,128)(2,1)S(1)} %reshape.172, bf16[1,1,7168,2048]{3,2,1,0:T(8,128)(2,1)} %param.14), kind=kOutput, calls=%fused_computation | convolution fusion | flops 1879048192 | bytes 30801920 | tf_op jit(solution)/shard_map/dot_general | solution.py:19
  70.2 28.6 %reduce-scatter.2.cloned.1.call-done = f32[8,2048]{1,0:T(8,128)} async-done(((f32[128,2048]{1,0:T(8,128)}), f32[8,2048]{1,0:T(8,128)}) %reduce-scatter.2.cloned.1.call-update) | async-done | bytes 65552 | tf_op jit(solution)/shard_map/reduce_scatter | solution.py:58
  98.8 0.8 fusion.34
  99.6 20.0 %all_gather.3 = bf16[128,1024]{1,0:T(8,128)(2,1)S(1)} all-gather(bf16[8,1024]{1,0:T(8,128)(2,1)S(1)} %fusion.34), channel_id=1, replica_groups=mesh['parts'=2,'expert'=16] {'expert'}, dimensions={0}, use_global_device_ids=true | all-gather | bytes 278528 | tf_op jit(solution)/shard_map/all_gather | solution.py:62
  119.6 1.6 convolution_convert_fusion.2
  121.2 0.8 copy.44
  122.0 3.5 %all-to-all-start.3 = ((bf16[16,8,448]{2,1,0:T(8,128)(2,1)}), bf16[16,8,448]{2,1,0:T(8,128)(2,1)S(1)}, u32[]{:S(2)}, u32[]{:S(2)}) async-start(bf16[16,8,448]{2,1,0:T(8,128)(2,1)} %bitcast.15), calls=%async_computation.4 | async-start | bytes 262144 | tf_op jit(solution)/shard_map/all_to_all | solution.py:66
  125.5 7.8 %fusion.2 = bf16[16,4,7168]{2,0,1:T(8,128)(2,1)S(1)} fusion(bf16[1,1,1024,7168]{3,2,1,0:T(8,128)(2,1)} %param.15, bf16[16,4,1024]{2,1,0:T(4,128)(2,1)S(1)} %dot_general.29), kind=kOutput, calls=%fused_computation.2 | convolution fusion | flops 939524096 | bytes 15728640 | tf_op jit(solution)/shard_map/dot_general | solution.py:23
  133.3 1.6 copy.41
  135.0 6.0 %all-to-all-start.1 = ((bf16[16,4,7168]{2,1,0:T(4,128)(2,1)}), bf16[16,4,7168]{2,1,0:T(4,128)(2,1)S(1)}, u32[]{:S(2)}, u32[]{:S(2)}) async-start(bf16[16,4,7168]{2,1,0:T(4,128)(2,1)} %copy.41), calls=%async_computation.1 | async-start | bytes 1835008 | tf_op jit(solution)/shard_map/all_to_all | solution.py:46
  141.0 0.7 select_reduce_fusion
  141.8 0.1 reshape.180
  141.9 0.1 reshape.179
  142.0 19.8 %all-to-all-done.1 = bf16[16,4,7168]{2,1,0:T(4,128)(2,1)S(1)} async-done(((bf16[16,4,7168]{2,1,0:T(4,128)(2,1)}), bf16[16,4,7168]{2,1,0:T(4,128)(2,1)S(1)}, u32[]{:S(2)}, u32[]{:S(2)}) %all-to-all-start.1) | async-done | bytes 917536 | tf_op jit(solution)/shard_map/all_to_all | solution.py:46
  161.7 1.4 fusion.45
  163.2 1.2 reshape.174
  164.4 0.2 reshape.173
  164.5 1.0 fusion.11
  165.5 1.0 fusion.10
  166.5 0.7 pad_maximum_fusion.2
  (31 shorter events, 1.1 us)
Async XLA Ops:
  6.5 28.9 %copy-start = (bf16[1,448,2048]{2,1,0:T(8,128)(2,1)S(1)}, bf16[1,448,2048]{2,1,0:T(8,128)(2,1)}, u32[]{:S(2)}) copy-start(bf16[1,448,2048]{2,1,0:T(8,128)(2,1)} %param.16) | copy-start | bytes 5505028
  11.8 17.5 %all-to-all-start.2 = ((bf16[8,16,448]{2,0,1:T(8,128)(2,1)}), bf16[8,16,448]{2,0,1:T(8,128)(2,1)S(1)}, u32[]{:S(2)}, u32[]{:S(2)}) async-start(bf16[8,16,448]{2,0,1:T(8,128)(2,1)} %pad_maximum_fusion.1), calls=%async_computation.2 | async-start | bytes 262144 | tf_op jit(solution)/shard_map/all_to_all | solution.py:56
  22.0 2.7 %copy-start.3 = (pred[4]{0:T(512)(128)(4,1)}, pred[4]{0:T(512)(128)(4,1)S(1)}, u32[]{:S(2)}) copy-start(pred[4]{0:T(512)(128)(4,1)S(1)} %iota_compare_fusion.5) | copy-start | bytes 16
  23.2 1.5 copy-start.4
  29.4 26.9 %all-to-all-start = ((bf16[16,4,7168]{2,1,0:T(4,128)(2,1)}), bf16[16,4,7168]{2,1,0:T(4,128)(2,1)}, u32[]{:S(2)}, u32[]{:S(2)}) async-start(bf16[16,4,7168]{2,1,0:T(4,128)(2,1)} %pad_maximum_fusion), calls=%async_computation | async-start | bytes 1835008 | tf_op jit(solution)/shard_map/all_to_all | solution.py:43
  35.4 63.4 %reduce-scatter.2.cloned.1.call-start = ((), (), s32[]{:S(2)}) async-start(), calls=%async_computation.5 | async-start | bytes 1114112 | tf_op jit(solution)/shard_map/reduce_scatter | solution.py:58
  70.0 70.9 %copy-start.2 = (f32[1,2,4,8]{3,2,1,0:T(4,128)S(1)}, f32[1,2,4,8]{3,2,1,0:T(4,128)}, u32[]{:S(2)}) copy-start(f32[1,2,4,8]{3,2,1,0:T(4,128)} %param.12) | copy-start | bytes 772
  70.0 94.5 %copy-start.1 = (bf16[2,4,7168]{2,1,0:T(4,128)(2,1)S(1)}, bf16[2,4,7168]{2,1,0:T(4,128)(2,1)}, u32[]{:S(2)}) copy-start(bf16[2,4,7168]{2,1,0:T(4,128)(2,1)} %param.9) | copy-start | bytes 344068
  122.0 13.0 %all-to-all-start.3 = ((bf16[16,8,448]{2,1,0:T(8,128)(2,1)}), bf16[16,8,448]{2,1,0:T(8,128)(2,1)S(1)}, u32[]{:S(2)}, u32[]{:S(2)}) async-start(bf16[16,8,448]{2,1,0:T(8,128)(2,1)} %bitcast.15), calls=%async_computation.4 | async-start | bytes 262144 | tf_op jit(solution)/shard_map/all_to_all | solution.py:66
  135.0 26.8 %all-to-all-start.1 = ((bf16[16,4,7168]{2,1,0:T(4,128)(2,1)}), bf16[16,4,7168]{2,1,0:T(4,128)(2,1)S(1)}, u32[]{:S(2)}, u32[]{:S(2)}) async-start(bf16[16,4,7168]{2,1,0:T(4,128)(2,1)} %copy.41), calls=%async_computation.1 | async-start | bytes 1835008 | tf_op jit(solution)/shard_map/all_to_all | solution.py:46
Sparse Core Ops, SparseCore 0:
  39.8 58.8 reduce-scatter.1
where the time goes:
time: 176 us; the launch traced here: 174 us
  waiting for transfers between devices  67.7 us (38%)
  matrix products  27.3 us (16%)
  starting transfers between devices  23 us (13%)
  blocking collectives  20 us (11%)
  between operations  13.7 us (8%)
  other arithmetic  11.4 us (6%)
  local copies, waits for them, and re-layouts  11.1 us (6%)
    reduce_scatter x1, waiting for transfers between devices, shared_block(): lax.psum_scatter(partial_value, 'expert', scatter_dimension=0, tiled=True)  28.6 us
    all_gather x1, blocking collectives, shared_block(): activated = lax.all_gather(own_active, 'expert', axis=0, tiled=True)  20 us
    all_to_all x1, waiting for transfers between devices, expert_repeat(): lax.all_to_all(results, 'expert', split_axis=0, concat_axis=0, tiled=True)  19.8 us
    all_to_all x1, waiting for transfers between devices, expert_repeat(): lax.all_to_all(copies, 'expert', split_axis=0, concat_axis=0, tiled=True)  19.3 us
    dot_general x1, matrix products, partial_swiglu(): projected = jnp.dot(inputs, gate_up, preferred_element_type=jnp.float32)  12.1 us
    dot_general x1, matrix products, partial_swiglu(): return jnp.dot(activated, down_proj, preferred_element_type=jnp.float32)  7.83 us
    all_to_all x1, starting transfers between devices, shared_block(): lax.all_to_all(stacked, 'expert', split_axis=1, concat_axis=0, tiled=True)  7.41 us
    all_to_all x1, starting transfers between devices, expert_repeat(): lax.all_to_all(copies, 'expert', split_axis=0, concat_axis=0, tiled=True)  6.05 us
  transfers between devices with their start and end apart: 5, of which 3 were waited for; matrix products, arithmetic and copies ran while one was open for 21% of the time, Pallas kernels for 0%

commit v1 on v0

v1 whole, which is shorter than its diff:
```python
import functools

import jax
import jax.numpy as jnp
from jax import lax
from jax.experimental import pallas as pl
from jax.experimental.pallas import tpu as pltpu
from jax.sharding import PartitionSpec as P

EXPERTS = 16
EPSILON = 1e-06
LANES = 128
BF16 = jnp.bfloat16
F32 = jnp.float32


def dotted(left, right):
    return jnp.dot(left, right, preferred_element_type=F32)


def layer_kernel(
    n,
    experts,
    group,
    chunk,
    window,
    tokens_ref,
    live_ref,
    ids_ref,
    gates_ref,
    gain_ref,
    gate_up_hbm,
    down_hbm,
    shared_up_hbm,
    shared_down_hbm,
    routed_out,
    shared_out,
    own_n,
    peer_n,
    x_all,
    gate_up,
    down,
    shared_up,
    shared_down,
    hidden,
    sh_part,
    sh_send,
    sh_peer,
    sh_y,
    sh_yr,
    sh_z,
    sh_zr,
    sh_hidden,
    so_send,
    so_recv,
    so_f,
    so_fr,
    part,
    r_p,
    r_pr,
    r_y,
    r_yr,
    r_z,
    r_zr,
    keep,
    res,
    res_r,
    w_sem,
    n_sem,
    xz_s,
    xy_s,
    xp_s,
    x_r,
    hz_s,
    hy_s,
    hp_s,
    h_r,
    sp_sem,
    sy_sem,
    sz_s,
    sz_r,
    so_s,
    so_r,
    p_s,
    p_r,
    y_s,
    y_r,
    z_s,
    z_r,
    f_sem,
):
    nc = n // 2
    na = nc // 2
    me = lax.axis_index("expert")
    c = lax.rem(me, 2)
    chip = lax.div(me, 2)
    b = lax.rem(chip, 2)
    a = lax.div(chip, 2)
    slot = b * na + a
    oc = 1 - c
    steps, rows_dev, width = tokens_ref.shape
    half = width // 2
    rows = steps * rows_dev
    pair = 2 * rows
    total_rows = nc * pair
    y_rows = na * pair
    units = down.shape[0]
    s_units = sh_part.shape[2]
    fb = shared_down.shape[1]

    def dev(a_at, b_at, c_at):
        return {"expert": (2 * a_at + b_at) * 2 + c_at}

    partner = dev(a, b, oc)
    across = dev(a, 1 - b, c)

    def rcopy(src, dst, send, recv, to):
        return pltpu.make_async_remote_copy(
            src_ref=src,
            dst_ref=dst,
            send_sem=send,
            recv_sem=recv,
            device_id=to,
            device_id_type=pl.DeviceIdType.MESH,
        )

    def a_of(d):
        return lax.rem(a + d, na)

    def a_from(d):
        return lax.rem(a + na - d, na)

    def block(at):
        return pl.ds(pl.multiple_of(at * pair, pair), pair)

    up_rows = width // 8
    loads = []
    offset = lax.rem(me, nc) * fb
    start = pl.multiple_of(lax.div(offset, LANES) * LANES, LANES)
    inner = pl.multiple_of(offset - start, 16)
    loads.append(
        pltpu.make_async_copy(
            shared_up_hbm.at[0], shared_up.at[pl.ds(inner, fb)], w_sem.at[0]
        )
    )
    loads.append(pltpu.make_async_copy(shared_down_hbm.at[0], shared_down, w_sem.at[1]))
    for at in range(8):
        piece = pl.ds(at * up_rows, up_rows)
        loads.append(
            pltpu.make_async_copy(
                gate_up_hbm.at[0, 0, piece], gate_up.at[piece], w_sem.at[2 + at]
            )
        )
    down_rows = units // 4
    for at in range(4):
        piece = pl.ds(at * down_rows, down_rows)
        loads.append(
            pltpu.make_async_copy(down_hbm.at[0, 0, piece], down.at[piece], w_sem.at[10 + at])
        )
    shared_up[...] = jnp.zeros_like(shared_up)

    barrier = pltpu.get_barrier_semaphore()

    def greet(to):
        pl.semaphore_signal(barrier, inc=1, device_id=to, device_id_type=pl.DeviceIdType.MESH)

    greet(partner)
    for d in range(1, nc):
        other = lax.rem(chip + d, nc)
        greet({"expert": other * 2 + c})
    for load in loads:
        load.start()

    lane = lax.broadcasted_iota(jnp.int32, (rows_dev, LANES), 1)
    row_at = lax.broadcasted_iota(jnp.int32, (rows_dev, LANES), 0)
    of_lane = lane & (experts - 1)
    level = lax.div(lane, experts)
    gain = gain_ref[...]
    for step in range(steps):
        h = tokens_ref[step].astype(F32)
        scaling = lax.rsqrt(jnp.mean(h * h, axis=-1, keepdims=True) + EPSILON)
        normed = (h * scaling * gain).astype(BF16).astype(F32)
        ids = ids_ref[0, step]
        gates = gates_ref[0, step]
        dense = jnp.zeros((rows_dev, LANES), F32)
        for k in range(ids.shape[1]):
            dense = dense + jnp.where(ids[:, k : k + 1] == of_lane, gates[:, k : k + 1], 0.0)
        dense = jnp.where(row_at < live_ref[step : step + 1, :], dense, 0.0)
        high = dense.astype(BF16).astype(F32)
        rest = dense - high
        mid = rest.astype(BF16).astype(F32)
        low = rest - mid
        coded = jnp.where(
            level == 0, high, jnp.where(level == 1, mid, jnp.where(level == 2, low, 0.0))
        )
        at = slice(step * rows_dev, (step + 1) * rows_dev)
        for side in range(2):
            own_n[side, at, :half] = normed[:, side * half : (side + 1) * half]
            own_n[side, at, half:] = coded

    pl.semaphore_wait(barrier, nc)

    swap = rcopy(own_n.at[oc], peer_n, n_sem.at[0], n_sem.at[1], partner)
    swap.start()
    swap.wait()
    mine = own_n[c]
    theirs = peer_n[...]
    first = jnp.where(c == 0, mine, theirs)
    second = jnp.where(c == 0, theirs, mine)
    x_all[c, block(slot)] = jnp.concatenate([first, second], axis=0).astype(BF16)

    def gather(buf, zs, ys, ps, rs):
        sent = []

        def push(at, send, to):
            copy = rcopy(buf.at[c, block(at)], buf.at[c, block(at)], send, rs.at[c, at], to)
            copy.start()
            sent.append(copy)

        def arrived(side, at):
            view = buf.at[side, block(at)]
            rcopy(view, view, ps.at[0], rs.at[side, at], partner).wait_recv()

        def begin():
            for d in range(1, na):
                push(slot, zs.at[d], dev(a_of(d), b, c))
            push(slot, ys.at[0], across)
            push(slot, ps.at[0], partner)

        def forward():
            for d in range(1, na):
                at = b * na + a_from(d)
                arrived(c, at)
                push(at, ys.at[d], across)
                push(at, ps.at[d], partner)

        def finish():
            for d in range(na):
                at = (1 - b) * na + a_from(d)
                arrived(c, at)
                push(at, ps.at[na + d], partner)
            for at in range(nc):
                arrived(oc, at)

        return begin, forward, finish, sent

    begin, forward, finish, sent = gather(x_all, xz_s, xy_s, xp_s, x_r)
    begin()
    forward()
    finish()
    pending = list(sent)

    expert = lax.div(me, group)
    codes = x_all[0, :, half:].astype(F32)
    wide = lax.broadcasted_iota(jnp.int32, (total_rows, LANES), 1) & (experts - 1)
    weight = jnp.sum(jnp.where(wide == expert, codes, 0.0), axis=1, keepdims=True)

    s_half = s_units // 2

    def shared_project():
        loads[0].wait()
        features = x_all[lax.div(me, nc), :, pl.ds(start, window)]
        for side in range(2):
            for kind in range(2):
                cols = slice(kind * s_units + side * s_half, kind * s_units + (side + 1) * s_half)
                sh_part[side, :, kind * s_half : (kind + 1) * s_half] = dotted(
                    features, shared_up[:, cols]
                )
        sh_send[...] = sh_part[oc].astype(BF16)
        copy = rcopy(sh_send, sh_peer, sp_sem.at[0], sp_sem.at[1], partner)
        copy.start()
        return copy

    y_own = pl.ds(pl.multiple_of(b * y_rows, y_rows), y_rows)
    y_other = pl.ds(pl.multiple_of((1 - b) * y_rows, y_rows), y_rows)

    def shared_across(copy):
        copy.wait()
        sh_y[...] = (sh_part[c, y_other] + sh_peer[y_other].astype(F32)).astype(BF16)
        out = rcopy(sh_y, sh_yr, sy_sem.at[0], sy_sem.at[1], across)
        out.start()
        return out

    def shared_along(copy):
        copy.wait()
        summed = sh_part[c, y_own] + sh_peer[y_own].astype(F32) + sh_yr[...].astype(F32)
        sh_part[0, :y_rows] = summed
        sh_z[...] = summed.astype(BF16).reshape(na, pair, s_units)
        copies = []
        for d in range(1, na):
            copy = rcopy(
                sh_z.at[a_of(d)],
                sh_zr.at[d],
                sz_s.at[d],
                sz_r.at[d],
                dev(a_of(d), b, c),
            )
            copy.start()
            copies.append(copy)
        return copies

    h_begin, h_forward, h_finish, h_sent = gather(sh_hidden, hz_s, hy_s, hp_s, h_r)

    def shared_active(copies):
        total = sh_part[0, block(a)]
        for d in range(1, na):
            copies[d - 1].wait()
            total = total + sh_zr[d].astype(F32)
        sh_hidden[c, block(slot)] = (
            jax.nn.silu(total[:, :s_half]) * total[:, s_half:]
        ).astype(BF16)
        h_begin()

    def shared_last():
        h_finish()
        pending.extend(h_sent)
        loads[1].wait()
        cols = dotted(sh_hidden[0], shared_down[:s_half]) + dotted(
            sh_hidden[1], shared_down[s_half:]
        )
        so_send[...] = cols.astype(BF16).reshape(nc, pair, fb)
        copies = []
        for d in range(1, nc):
            other = lax.rem(chip + d, nc)
            to_slot = lax.rem(other, 2) * na + lax.div(other, 2)
            copy = rcopy(
                so_send.at[to_slot],
                so_recv.at[chip],
                so_s.at[d],
                so_r.at[chip],
                {"expert": other * 2 + c},
            )
            copy.start()
            copies.append(copy)
        return copies

    def shared_collect(copies):
        for d in range(1, nc):
            other = lax.rem(chip + nc - d, nc)
            view = so_recv.at[other]
            rcopy(view, view, so_s.at[0], so_r.at[other], partner).wait_recv()
        so_recv[chip] = so_send[slot]
        for at in range(nc):
            value = so_recv[at].astype(F32)
            so_f[0, at] = value[:rows]
            so_f[1, at] = value[rows:]
        copy = rcopy(so_f.at[oc], so_fr, f_sem.at[2], f_sem.at[3], partner)
        copy.start()
        for copy_at in copies:
            copy_at.wait_send()
        return copy

    def gate_up_tile(at, tile):
        def product(first_col):
            cols = slice(first_col, first_col + tile)
            return dotted(x_all[0, :, :half], gate_up[:half, cols]) + dotted(
                x_all[1, :, :half], gate_up[half:, cols]
            )

        gate = product(at * tile)
        up = product(units + at * tile)
        hidden[:, at * tile : (at + 1) * tile] = (jax.nn.silu(gate) * up).astype(BF16)

    state = [shared_project()]
    for load in loads[2:10]:
        load.wait()
    tile = min(256, units)
    stages = [
        lambda: state.append(shared_across(state[-1])),
        lambda: state.append(shared_along(state[-1])),
        lambda: shared_active(state[-1]),
        lambda: h_forward(),
    ]
    for at in range(units // tile):
        gate_up_tile(at, tile)
        if stages:
            stages.pop(0)()
    for stage in stages:
        stage()
    for load in loads[10:]:
        load.wait()

    chunks = half // chunk

    def product(side, j):
        cols = pl.ds(pl.multiple_of(side * half + j * chunk, LANES), chunk)
        return dotted(hidden[...], down[:, cols]) * weight

    to_partner = []
    for j in range(chunks):
        r_p[j] = product(oc, j).astype(BF16)
        copy = rcopy(r_p.at[j], r_pr.at[j], p_s.at[j], p_r.at[j], partner)
        copy.start()
        to_partner.append(copy)
    so_copies = shared_last()

    to_across = []
    to_along = []

    def send_across(j):
        part[...] = product(c, j)
        to_partner[j].wait()
        r_y[j] = (part[y_other] + r_pr[j, y_other].astype(F32)).astype(BF16)
        copy = rcopy(r_y.at[j], r_yr.at[j], y_s.at[j], y_r.at[j], across)
        copy.start()
        to_across.append(copy)
        keep[j] = part[y_own] + r_pr[j, y_own].astype(F32)

    def send_along(j):
        to_across[j].wait()
        summed = keep[j] + r_yr[j].astype(F32)
        r_z[j] = summed.astype(BF16).reshape(na, pair, chunk)
        copies = []
        for d in range(1, na):
            copy = rcopy(
                r_z.at[j, a_of(d)],
                r_zr.at[j, d],
                z_s.at[j, d],
                z_r.at[j, d],
                dev(a_of(d), b, c),
            )
            copy.start()
            copies.append(copy)
        to_along.append(copies)
        keep[j] = summed

    def collect(j):
        total = keep[j, block(a)]
        for d in range(1, na):
            to_along[j][d - 1].wait()
            total = total + r_zr[j, d].astype(F32)
        cols = slice(j * chunk, (j + 1) * chunk)
        res[0, :, cols] = total[:rows]
        res[1, :, cols] = total[rows:]

    for j in range(chunks):
        send_across(j)
        if j >= 2:
            send_along(j - 2)
    for j in range(max(chunks - 2, 0), chunks):
        send_along(j)
    shared_swap = shared_collect(so_copies)
    for j in range(chunks):
        collect(j)
    last = rcopy(res.at[oc], res_r, f_sem.at[0], f_sem.at[1], partner)
    last.start()
    own_cols = pl.ds(pl.multiple_of(c * half, LANES), half)
    other_cols = pl.ds(pl.multiple_of(oc * half, LANES), half)
    routed_out[:, own_cols] = res[c]
    shared_swap.wait()
    shared_out[c] = so_f[c]
    shared_out[oc] = so_fr[...]
    last.wait()
    routed_out[:, other_cols] = res_r[...]
    for copy in pending:
        copy.wait_send()


def per_device(
    tokens,
    live_rows,
    expert_ids,
    gate_weights,
    norm_gain,
    expert_gate_up,
    expert_down,
    shared_gate_up,
    shared_down,
):
    step_count, row_count, model_width = tokens.shape
    n = lax.axis_size("expert")
    group = n // EXPERTS
    units = expert_down.shape[2]
    fb, s_wide = shared_gate_up.shape[1:]
    s_units = s_wide // 2
    nc = n // 2
    na = nc // 2
    half = model_width // 2
    rows = step_count * row_count
    pair = 2 * rows
    total = nc * pair
    y_rows = na * pair
    wide = half + LANES
    chunk = next(size for size in (512, 256, 128) if half % size == 0)
    chunks = half // chunk
    span = next(size for size in (128, 64, 32, 16) if fb % size == 0)
    window = -(-(fb + LANES - span) // LANES) * LANES
    dma = pltpu.SemaphoreType.DMA
    vmem = pltpu.VMEM
    whole = pl.BlockSpec(memory_space=pltpu.VMEM)
    anywhere = pl.BlockSpec(memory_space=pl.ANY)
    routed, shared = pl.pallas_call(
        functools.partial(layer_kernel, n, EXPERTS, group, chunk, window),
        out_shape=(
            jax.ShapeDtypeStruct((rows, model_width), F32),
            jax.ShapeDtypeStruct((2, nc, rows, fb), F32),
        ),
        in_specs=[whole] * 5 + [anywhere] * 4,
        out_specs=(whole, whole),
        scratch_shapes=[
            vmem((2, rows, wide), F32),
            vmem((rows, wide), F32),
            vmem((2, total, wide), BF16),
            vmem((model_width, 2 * units), BF16),
            vmem((units, model_width), BF16),
            vmem((window, s_wide), BF16),
            vmem((s_units, fb), BF16),
            vmem((total, units), BF16),
            vmem((2, total, s_units), F32),
            vmem((total, s_units), BF16),
            vmem((total, s_units), BF16),
            vmem((y_rows, s_units), BF16),
            vmem((y_rows, s_units), BF16),
            vmem((na, pair, s_units), BF16),
            vmem((na, pair, s_units), BF16),
            vmem((2, total, s_units // 2), BF16),
            vmem((nc, pair, fb), BF16),
            vmem((nc, pair, fb), BF16),
            vmem((2, nc, rows, fb), F32),
            vmem((nc, rows, fb), F32),
            vmem((total, chunk), F32),
            vmem((chunks, total, chunk), BF16),
            vmem((chunks, total, chunk), BF16),
            vmem((chunks, y_rows, chunk), BF16),
            vmem((chunks, y_rows, chunk), BF16),
            vmem((chunks, na, pair, chunk), BF16),
            vmem((chunks, na, pair, chunk), BF16),
            vmem((chunks, y_rows, chunk), F32),
            vmem((2, rows, half), F32),
            vmem((rows, half), F32),
            dma((14,)),
            dma((2,)),
            dma((na,)),
            dma((na,)),
            dma((nc,)),
            dma((2, nc)),
            dma((na,)),
            dma((na,)),
            dma((nc,)),
            dma((2, nc)),
            dma((2,)),
            dma((2,)),
            dma((na,)),
            dma((na,)),
            dma((nc,)),
            dma((nc,)),
            dma((chunks,)),
            dma((chunks,)),
            dma((chunks,)),
            dma((chunks,)),
            dma((chunks, na)),
            dma((chunks, na)),
            dma((4,)),
        ],
        compiler_params=pltpu.CompilerParams(
            collective_id=0, has_side_effects=True, vmem_limit_bytes=67_043_328
        ),
    )(
        tokens,
        live_rows,
        expert_ids,
        gate_weights,
        norm_gain,
        expert_gate_up,
        expert_down,
        shared_gate_up,
        shared_down,
    )
    shared = jnp.transpose(shared, (2, 1, 0, 3)).reshape(step_count, row_count, model_width)
    routed = routed.reshape(step_count, row_count, model_width)
    live = jnp.arange(row_count, dtype=jnp.int32)[None, :] < live_rows
    update = jnp.where(live[:, :, None], routed + shared, 0.0)
    return (tokens.astype(F32) + update).astype(BF16)


def solution(mesh):
    placed = (
        P(None, ("parts", "expert"), None),
        P(None, ("parts", "expert")),
        P(None, None, ("parts", "expert"), None),
        P(None, None, ("parts", "expert"), None),
        P(),
        P(None, "expert", None, None),
        P(None, "expert", None, None),
        P(None, "expert", None),
        P(None, None, "expert"),
    )
    return jax.shard_map(
        per_device,
        mesh=mesh,
        in_specs=placed,
        out_specs=P(None, ("parts", "expert"), None),
        check_vma=False,
    )
```

time: 176 us -> 75.8 us (0.43)
  waiting for transfers between devices: 67.7 us -> 0 us
  Pallas kernels: 0 us -> 67 us
  matrix products: 27.3 us -> 0 us
  starting transfers between devices: 23 us -> 0 us
  blocking collectives: 20 us -> 0 us
  between operations: 13.7 us -> 0.02 us
  other arithmetic: 11.4 us -> 2.41 us
  local copies, waits for them, and re-layouts: 11.1 us -> 6.07 us
    pallas_call x0 -> x1, Pallas kernels: none -> 67 us  [per_device(): pl.pallas_call(functools.partial(layer_kernel, n, EXPERTS, group, chunk,...]
    all_to_all x4 -> x0, waiting for transfers between devices: 39.1 us -> none  [the longest x1 19.8 us: expert_repeat(): lax.all_to_all(results, 'expert', split_axis=0, concat_axis=0, tiled=True)]
    reduce_scatter x1 -> x0, waiting for transfers between devices: 28.6 us -> none  [shared_block(): lax.psum_scatter(partial_value, 'expert', scatter_dimension=0, tiled=True)]
    dot_general x8 -> x0, matrix products: 27.3 us -> none  [the longest x1 12.1 us: partial_swiglu(): projected = jnp.dot(inputs, gate_up, preferred_element_type=jnp.float32)]
    all_to_all x4 -> x0, starting transfers between devices: 23 us -> none  [the longest x1 7.41 us: shared_block(): lax.all_to_all(stacked, 'expert', split_axis=1, concat_axis=0, tiled=True)]
    all_gather x1 -> x0, blocking collectives: 20 us -> none  [shared_block(): activated = lax.all_gather(own_active, 'expert', axis=0, tiled=True)]
    slice x3 -> x0, local copies, waits for them, and re-layouts: 3.42 us -> none  [the longest x1 1.41 us: per_device(): returned[:, step_at * capacity:(step_at + 1) * capacity]]
    unnamed x11 -> x2, local copies, waits for them, and re-layouts: 0.54 us -> 3.55 us
  transfers between devices with their start and end apart: 5 -> 0, of which waited for: 3 -> 0; matrix products, arithmetic and copies ran while one was open for 21% -> 0% of each run, Pallas kernels for 0% -> 0%
where the time goes in v1:
time: 75.8 us; the launch traced here: 75.5 us
  Pallas kernels  67 us (88%)
  local copies, waits for them, and re-layouts  6.07 us (8%)
  other arithmetic  2.41 us (3%)
    pallas_call x1, Pallas kernels, per_device(): pl.pallas_call(functools.partial(layer_kernel, n, EXPERTS, group, chunk,...  67 us
    unnamed x2, local copies, waits for them, and re-layouts  3.55 us
    convert_element_type x1, other arithmetic, per_device(): return (tokens.astype(F32) + update).astype(BF16)  1.68 us

profile of v1, /device:TPU:0, one launch (start us, length us, event | category | flops | bytes accessed | tf_op | source)
XLA Modules:
  0.0 75.5 jit_solution(13550034734981689315)
XLA Ops:
  0.0 2.3 %copy.13.shared_down_hbm = bf16[1,1024,448]{2,1,0:T(8,128)(2,1)} copy(bf16[1,1024,448]{1,2,0:T(8,128)(2,1)} %param.17) | data formatting | bytes 1835008 | tf_op args[8]
  2.3 1.3 %copy.12.live_ref = s32[2,1]{1,0:T(2,128)} copy(s32[2,1]{0,1:T(1,128)} %param.10) | data formatting | bytes 16 | tf_op args[1]
  3.6 67.0 %shard_map.94 = (f32[8,7168]{1,0:T(8,128)}, f32[2,8,8,448]{3,2,1,0:T(8,128)}) custom-call(bf16[2,4,7168]{2,1,0:T(4,128)(2,1)} %tokens_ref.1, s32[2,1]{1,0:T(2,128)} %copy.12.live_ref, s32[1,2,4,8]{3,2,1,0:T(4,128)} %ids_ref.1, f32[1,2,4,8]{3,2,1,0:T(4,128)} %gates_ref.1, f32[1,7168]{1,0:T(1,128)} %gain_ref.1, bf16[1,1,7168,2048]{3,2,1,0:T(8,128)(2,1)} %gate_up_hbm.1, ...), custom_call_target="tpu_custom_call" | custom-call | tf_op jit(solution)/shard_map/pallas_call | solution.py:492
  70.6 1.2 %copy.14 = f32[8,8,2,448]{3,2,1,0:T(2,128)S(1)} copy(f32[8,8,2,448]{3,0,1,2:T(8,128)} %bitcast.2) | data formatting | bytes 458752 | tf_op jit(solution)/shard_map/transpose | solution.py:569
  71.7 0.4 reshape.29
  72.1 1.0 %reshape.28 = f32[2,4,7168]{2,1,0:T(4,128)S(1)} reshape(f32[8,7168]{1,0:T(8,128)} %get-tuple-element.7) | data formatting | bytes 458752 | tf_op jit(solution)/shard_map/reshape | solution.py:570
  73.1 0.7 iota_compare_fusion
  73.8 1.7 %add_convert_fusion = bf16[2,4,7168]{2,1,0:T(4,128)(2,1)} fusion(f32[2,4,7168]{2,1,0:T(4,128)S(1)} %reshape.28, f32[2,4,7168]{2,1,0:T(4,128)S(1)} %reshape.29, bf16[2,4,7168]{2,1,0:T(4,128)(2,1)} %tokens_ref.1, pred[2,4]{1,0:T(4,128)(4,1)S(1)} %iota_compare_fusion), kind=kLoop, calls=%fused_computation | loop fusion | flops 286720 | bytes 688136 | tf_op jit(solution)/shard_map/convert_element_type | solution.py:573

commit v2 on v1

--- a/solution.py
+++ b/solution.py
@@ -16,6 +16,10 @@
 
 def dotted(left, right):
     return jnp.dot(left, right, preferred_element_type=F32)
+
+
+def dotted_nt(left, right):
+    return lax.dot_general(left, right, (((1,), (1,)), ((), ())), preferred_element_type=F32)
 
 
 def layer_kernel(
@@ -33,8 +37,8 @@
     down_hbm,
     shared_up_hbm,
     shared_down_hbm,
-    routed_out,
-    shared_out,
+    update_out,
+    acc,
     own_n,
     peer_n,
     x_all,
@@ -106,7 +110,7 @@
     y_rows = na * pair
     units = down.shape[0]
     s_units = sh_part.shape[2]
-    fb = shared_down.shape[1]
+    fb = shared_down.shape[0]
 
     def dev(a_at, b_at, c_at):
         return {"expert": (2 * a_at + b_at) * 2 + c_at}
@@ -185,7 +189,7 @@
         dense = jnp.zeros((rows_dev, LANES), F32)
         for k in range(ids.shape[1]):
             dense = dense + jnp.where(ids[:, k : k + 1] == of_lane, gates[:, k : k + 1], 0.0)
-        dense = jnp.where(row_at < live_ref[step : step + 1, :], dense, 0.0)
+        dense = jnp.where(row_at < live_ref[:, step : step + 1], dense, 0.0)
         high = dense.astype(BF16).astype(F32)
         rest = dense - high
         mid = rest.astype(BF16).astype(F32)
@@ -315,8 +319,8 @@
         h_finish()
         pending.extend(h_sent)
         loads[1].wait()
-        cols = dotted(sh_hidden[0], shared_down[:s_half]) + dotted(
-            sh_hidden[1], shared_down[s_half:]
+        cols = dotted_nt(sh_hidden[0], shared_down[:, :s_half]) + dotted_nt(
+            sh_hidden[1], shared_down[:, s_half:]
         )
         so_send[...] = cols.astype(BF16).reshape(nc, pair, fb)
         copies = []
@@ -365,18 +369,10 @@
     for load in loads[2:10]:
         load.wait()
     tile = min(256, units)
-    stages = [
-        lambda: state.append(shared_across(state[-1])),
-        lambda: state.append(shared_along(state[-1])),
-        lambda: shared_active(state[-1]),
-        lambda: h_forward(),
-    ]
     for at in range(units // tile):
         gate_up_tile(at, tile)
-        if stages:
-            stages.pop(0)()
-    for stage in stages:
-        stage()
+        if at == 0:
+            state.append(shared_across(state[-1]))
     for load in loads[10:]:
         load.wait()
 
@@ -387,12 +383,12 @@
         return dotted(hidden[...], down[:, cols]) * weight
 
     to_partner = []
-    for j in range(chunks):
+
+    def send_partner(j):
         r_p[j] = product(oc, j).astype(BF16)
         copy = rcopy(r_p.at[j], r_pr.at[j], p_s.at[j], p_r.at[j], partner)
         copy.start()
         to_partner.append(copy)
-    so_copies = shared_last()
 
     to_across = []
     to_along = []
@@ -433,12 +429,26 @@
         res[0, :, cols] = total[:rows]
         res[1, :, cols] = total[rows:]
 
-    for j in range(chunks):
-        send_across(j)
-        if j >= 2:
+    stages = {
+        0: lambda: state.append(shared_along(state[-1])),
+        2: lambda: shared_active(state[-1]),
+        4: h_forward,
+        5: lambda: state.append(shared_last()),
+    }
+    for j in range(min(2, chunks)):
+        send_partner(j)
+    for j in range(max(chunks, 6)):
+        if j + 2 < chunks:
+            send_partner(j + 2)
+        if j < chunks:
+            send_across(j)
+        if 2 <= j and j - 2 < chunks:
             send_along(j - 2)
-    for j in range(max(chunks - 2, 0), chunks):
+        if j in stages:
+            stages[j]()
+    for j in range(max(chunks, 6) - 2, chunks):
         send_along(j)
+    so_copies = state[-1]
     shared_swap = shared_collect(so_copies)
     for j in range(chunks):
         collect(j)
@@ -446,12 +456,18 @@
     last.start()
     own_cols = pl.ds(pl.multiple_of(c * half, LANES), half)
     other_cols = pl.ds(pl.multiple_of(oc * half, LANES), half)
-    routed_out[:, own_cols] = res[c]
+    acc[:, own_cols] = res[c]
     shared_swap.wait()
-    shared_out[c] = so_f[c]
-    shared_out[oc] = so_fr[...]
     last.wait()
-    routed_out[:, other_cols] = res_r[...]
+    acc[:, other_cols] = res_r[...]
+    for at in range(nc):
+        slot_chip = so_f[c, at]
+        peer_chip = so_fr[at]
+        for side in range(2):
+            cols = slice((2 * at + side) * fb, (2 * at + side + 1) * fb)
+            acc[:, cols] = acc[:, cols] + jnp.where(c == side, slot_chip, peer_chip)
+    for step in range(steps):
+        update_out[step] = acc[step * rows_dev : (step + 1) * rows_dev]
     for copy in pending:
         copy.wait_send()
 
@@ -489,22 +505,20 @@
     vmem = pltpu.VMEM
     whole = pl.BlockSpec(memory_space=pltpu.VMEM)
     anywhere = pl.BlockSpec(memory_space=pl.ANY)
-    routed, shared = pl.pallas_call(
+    update = pl.pallas_call(
         functools.partial(layer_kernel, n, EXPERTS, group, chunk, window),
-        out_shape=(
-            jax.ShapeDtypeStruct((rows, model_width), F32),
-            jax.ShapeDtypeStruct((2, nc, rows, fb), F32),
-        ),
+        out_shape=jax.ShapeDtypeStruct(tokens.shape, F32),
         in_specs=[whole] * 5 + [anywhere] * 4,
-        out_specs=(whole, whole),
+        out_specs=whole,
         scratch_shapes=[
+            vmem((rows, model_width), F32),
             vmem((2, rows, wide), F32),
             vmem((rows, wide), F32),
             vmem((2, total, wide), BF16),
             vmem((model_width, 2 * units), BF16),
             vmem((units, model_width), BF16),
             vmem((window, s_wide), BF16),
-            vmem((s_units, fb), BF16),
+            vmem((fb, s_units), BF16),
             vmem((total, units), BF16),
             vmem((2, total, s_units), F32),
             vmem((total, s_units), BF16),
@@ -557,19 +571,17 @@
         ),
     )(
         tokens,
-        live_rows,
+        live_rows.T,
         expert_ids,
         gate_weights,
         norm_gain,
         expert_gate_up,
         expert_down,
         shared_gate_up,
-        shared_down,
+        jnp.swapaxes(shared_down, 1, 2),
     )
-    shared = jnp.transpose(shared, (2, 1, 0, 3)).reshape(step_count, row_count, model_width)
-    routed = routed.reshape(step_count, row_count, model_width)
     live = jnp.arange(row_count, dtype=jnp.int32)[None, :] < live_rows
-    update = jnp.where(live[:, :, None], routed + shared, 0.0)
+    update = jnp.where(live[:, :, None], update, 0.0)
     return (tokens.astype(F32) + update).astype(BF16)
 
 

time: 75.8 us -> 63 us (0.83)
  Pallas kernels: 67 us -> 59.9 us
  local copies, waits for them, and re-layouts: 6.07 us -> 0 us
    pallas_call x1, Pallas kernels: 67 us -> 59.9 us  [per_device(): pl.pallas_call(functools.partial(layer_kernel, n, EXPERTS, group, chunk,...]
    unnamed x2 -> x0, local copies, waits for them, and re-layouts: 3.55 us -> none
    reshape x2 -> x0, local copies, waits for them, and re-layouts: 1.37 us -> none  [the longest x1 1.01 us: per_device(): routed = routed.reshape(step_count, row_count, model_width)]
    transpose x1 -> x0, local copies, waits for them, and re-layouts: 1.15 us -> none  [per_device(): jnp.transpose(shared, (2, 1, 0, 3))]
where the time goes in v2:
time: 63 us; the launch traced here: 62.9 us
  Pallas kernels  59.9 us (95%)
  other arithmetic  3.01 us (5%)
    pallas_call x1, Pallas kernels, per_device(): pl.pallas_call(functools.partial(layer_kernel, n, EXPERTS, group, chunk,...  59.9 us
    convert_element_type x1, other arithmetic, per_device(): return (tokens.astype(F32) + update).astype(BF16)  1.77 us

profile of v2, /device:TPU:0, one launch (start us, length us, event | category | flops | bytes accessed | tf_op | source)
XLA Modules:
  0.0 62.9 jit_solution(16477742760913149487)
XLA Ops:
  0.0 1.2 %iota_compare_fusion = pred[2,4]{1,0:T(4,128)(4,1)} fusion(s32[2]{0:T(128)} %bitcast.4), kind=kLoop, calls=%fused_computation.1 | loop fusion | flops 8 | bytes 16 | tf_op jit(solution)/shard_map/lt | solution.py:583
  1.2 59.9 %shard_map.94 = f32[2,4,7168]{2,1,0:T(4,128)} custom-call(bf16[2,4,7168]{2,1,0:T(4,128)(2,1)} %tokens_ref.1, s32[1,2]{1,0:T(1,128)} %bitcast.5, s32[1,2,4,8]{3,2,1,0:T(4,128)} %ids_ref.1, f32[1,2,4,8]{3,2,1,0:T(4,128)} %gates_ref.1, f32[1,7168]{1,0:T(1,128)} %gain_ref.1, bf16[1,1,7168,2048]{3,2,1,0:T(8,128)(2,1)} %gate_up_hbm.1, ...), custom_call_target="tpu_custom_call" | custom-call | tf_op jit(solution)/shard_map/pallas_call | solution.py:508
  61.1 1.8 %add_convert_fusion = bf16[2,4,7168]{2,1,0:T(4,128)(2,1)} fusion(f32[2,4,7168]{2,1,0:T(4,128)} %shard_map.94, bf16[2,4,7168]{2,1,0:T(4,128)(2,1)} %tokens_ref.1, pred[2,4]{1,0:T(4,128)(4,1)} %iota_compare_fusion), kind=kLoop, calls=%fused_computation | loop fusion | flops 229376 | bytes 458760 | tf_op jit(solution)/shard_map/convert_element_type | solution.py:585
